TPU v7x, 32 devices: a whole 2x2x4 slice. The times are simulated.
32 devices in a mesh: row: 4 (over y, x), col: 4 (over z), crop: 2 (over core).
Axes of the slice: x: 2, y: 2, z: 4, core: 2. Of those that a mesh axis runs over, the one named last changes fastest.
Arguments:
- pair_repr: bfloat16 [256, 128, 128], P(('crop', 'row'), 'col'), parts along dimension 0, may hold values from -6 to 6
- pair_mask: int32 [256, 128], P(('crop', 'row'), 'col'), parts along dimension 0, may hold values 0 or 1
- out_left_w: bfloat16 [128, 256], replicated, may hold values from -0.5 to 0.5
- out_right_w: bfloat16 [128, 256], replicated, may hold values from -0.5 to 0.5
- out_gate_w: bfloat16 [128, 128], replicated, may hold values from -0.5 to 0.5
- out_final_w: bfloat16 [128, 128], replicated, may hold values from -0.5 to 0.5
- in_left_w: bfloat16 [128, 256], replicated, may hold values from -0.5 to 0.5
- in_right_w: bfloat16 [128, 256], replicated, may hold values from -0.5 to 0.5
- in_gate_w: bfloat16 [128, 128], replicated, may hold values from -0.5 to 0.5
- in_final_w: bfloat16 [128, 128], replicated, may hold values from -0.5 to 0.5
- trans_in_w: bfloat16 [128, 1024], replicated, may hold values from -0.5 to 0.5
- trans_out_w: bfloat16 [512, 128], replicated, may hold values from -0.25 to 0.25
Outputs:
- pair_out: bfloat16 [256, 128, 128], P(('crop', 'row'), 'col'), parts along dimension 0
There are 2 independent parts, one for each index of `crop`. A program takes and returns all parts, laid end to end along the dimension named above; an argument that names none is the same for every part. Nothing has to cross between parts.
All inputs are finite; a program needn't handle non-finite values. No bound on the sum of `pair_mask` on one device may be relied on, other than what follows from the above.
Results may differ from a plain program's by a relative error of at most 0.015.
Values may be sent and summed in bfloat16 or wider, within the bound.
No kernel may reach another device: no remote copies, remote signals or barrier semaphores. Data moves between devices by JAX's collectives and lax.ppermute only.
A program may use at most 128 MiB of HBM per device.

v0:
```python
import jax
import jax.numpy as jnp
from jax import lax
from jax.sharding import PartitionSpec as P

epsilon = 1e-05


def layer_norm(values):
    average = jnp.mean(values, axis=-1, keepdims=True)
    centered = values - average
    spread = jnp.mean(centered * centered, axis=-1, keepdims=True)
    return centered * lax.rsqrt(spread + epsilon)


def gated(normed, weight, mask_vals):
    projected = jnp.dot(normed, weight, preferred_element_type=jnp.float32)
    half_width = weight.shape[1] // 2
    result = jax.nn.sigmoid(projected[..., :half_width]) * projected[..., half_width:]
    result = result * mask_vals[..., None]
    return result.astype(jnp.bfloat16)


def finish(pair_repr, normed, triangle, gate_w, final_w):
    gate_vals = jax.nn.sigmoid(jnp.dot(normed, gate_w, preferred_element_type=jnp.float32))
    tri_norm = layer_norm(triangle).astype(jnp.bfloat16)
    update = jnp.dot(tri_norm, final_w, preferred_element_type=jnp.float32)
    return (pair_repr.astype(jnp.float32) + gate_vals * update).astype(jnp.bfloat16)


def shards(
    pair_repr,
    pair_mask,
    out_left_w,
    out_right_w,
    out_gate_w,
    out_final_w,
    in_left_w,
    in_right_w,
    in_gate_w,
    in_final_w,
    trans_in_w,
    trans_out_w,
):
    mask_vals = pair_mask.astype(jnp.float32)
    normed_out = layer_norm(pair_repr.astype(jnp.float32)).astype(jnp.bfloat16)
    outbound = gated(normed_out, out_right_w, mask_vals)
    turned_right = lax.all_to_all(
        lax.all_to_all(outbound, "row", split_axis=0, concat_axis=0, tiled=True),
        "col",
        split_axis=0,
        concat_axis=1,
        tiled=True,
    )
    left_tile = gated(normed_out, out_left_w, mask_vals)
    gathered = lax.all_gather(left_tile, "col", axis=1, tiled=True)
    triangle = jnp.einsum(
        "ikh,jkh->ijh",
        gathered,
        lax.all_gather(turned_right, "row", axis=0, tiled=True),
        preferred_element_type=jnp.float32,
    )
    middle = finish(pair_repr, normed_out, triangle, out_gate_w, out_final_w)
    normed_in = layer_norm(middle.astype(jnp.float32)).astype(jnp.bfloat16)
    outbound_left = gated(normed_in, in_left_w, mask_vals)
    turned_left = lax.all_to_all(
        lax.all_to_all(outbound_left, "col", split_axis=1, concat_axis=1, tiled=True),
        "row",
        split_axis=1,
        concat_axis=0,
        tiled=True,
    )
    right_tile = gated(normed_in, in_right_w, mask_vals)
    column_panel = lax.all_gather(right_tile, "row", axis=0, tiled=True)
    triangle_in = jnp.einsum(
        "kih,kjh->ijh",
        lax.all_gather(turned_left, "col", axis=1, tiled=True),
        column_panel,
        preferred_element_type=jnp.float32,
    )
    after_in = finish(middle, normed_in, triangle_in, in_gate_w, in_final_w)
    normed_mix = layer_norm(after_in.astype(jnp.float32)).astype(jnp.bfloat16)
    projected = jnp.dot(normed_mix, trans_in_w, preferred_element_type=jnp.float32)
    half_width = trans_in_w.shape[1] // 2
    hidden = (jax.nn.silu(projected[..., :half_width]) * projected[..., half_width:]).astype(
        jnp.bfloat16
    )
    result = after_in.astype(jnp.float32) + jnp.dot(
        hidden, trans_out_w, preferred_element_type=jnp.float32
    )
    return result.astype(jnp.bfloat16)


def solution(mesh):
    in_specs = (
        P(("crop", "row"), "col", None),
        P(("crop", "row"), "col"),
        P(),
        P(),
        P(),
        P(),
        P(),
        P(),
        P(),
        P(),
        P(),
        P(),
    )
    out_specs = P(("crop", "row"), "col", None)
    return jax.shard_map(shards, mesh=mesh, in_specs=in_specs, out_specs=out_specs, check_vma=False)
```

profile of v0, /device:TPU:0, one launch (start us, length us, event | category | flops | bytes accessed | tf_op | source)
XLA Modules:
  0.0 162.0 jit_solution(13725264176336256992)
XLA Ops:
  6.5 1.2 convert_reduce_fusion
  7.8 1.3 fusion.17
  9.1 1.4 fusion.44
  10.6 1.3 fusion.46
  11.9 1.0 fusion.30
  13.0 10.7 %all_to_all.46 = bf16[32,32,128]{2,1,0:T(8,128)(2,1)S(1)} all-to-all(bf16[32,32,128]{2,1,0:T(8,128)(2,1)S(1)} %get-tuple-element.8), channel_id=1, replica_groups=mesh['row'=4,'col'=4,'crop'=2] {'row'}, dimensions={0} | all-to-all | bytes 524288 | tf_op jit(solution)/shard_map/all_to_all | solution.py:49
  23.7 21.0 %all_to_all.47 = bf16[32,32,128]{2,1,0:T(8,128)(2,1)S(1)} all-to-all(bf16[32,32,128]{2,1,0:T(8,128)(2,1)S(1)} %all_to_all.46), channel_id=1, replica_groups=mesh['row'=4,'col'=4,'crop'=2] {'col'}, dimensions={0} | all-to-all | bytes 524288 | tf_op jit(solution)/shard_map/all_to_all | solution.py:48
  44.7 0.9 copy.66
  45.7 0.7 fusion.6
  46.5 3.4 %all-gather.7.cloned.1.call-done = bf16[32,128,128]{2,1,0:T(8,128)(2,1)} async-done(((bf16[32,32,128]{2,1,0:T(8,128)(2,1)}), bf16[32,128,128]{2,1,0:T(8,128)(2,1)}) %all-gather.7.cloned.1.call-update) | async-done | bytes 1048592 | tf_op jit(solution)/shard_map/all_gather | solution.py:56
  49.9 2.7 %copy.67 = bf16[32,128,128]{1,0,2:T(8,128)(2,1)} copy(bf16[32,128,128]{2,1,0:T(8,128)(2,1)} %all-gather.7.cloned.1.call-done) | data formatting | bytes 2097152 | tf_op jit(solution)/shard_map/all_gather | solution.py:56
  52.5 24.4 %all-gather.5.cloned.1.call-done = bf16[32,128,128]{1,0,2:T(8,128)(2,1)} async-done(((bf16[8,128,128]{1,0,2:T(8,128)(2,1)}), bf16[32,128,128]{1,0,2:T(8,128)(2,1)}) %all-gather.5.cloned.1.call-update) | async-done | bytes 1048592 | tf_op jit(solution)/shard_map/all_gather | solution.py:60
  76.9 2.2 %bitcast_reduce_fusion.1 = (f32[32,32]{0,1:T(8,128)S(1)}, f32[128,32,32]{2,1,0:T(8,128)S(1)}) fusion(bf16[32,128,128]{1,0,2:T(8,128)(2,1)} %all-gather.5.cloned.1.call-done, bf16[32,128,128]{1,0,2:T(8,128)(2,1)} %copy.67), kind=kOutput, calls=%fused_computation.5 | convolution fusion | flops 33684480 | bytes 2625536 | tf_op jit(solution)/shard_map/ikh,jkh->ijh/dot_general | solution.py:57
  79.2 0.1 copy.68
  79.2 0.1 copy.69
  79.3 0.3 multiply_reduce_fusion.1
  79.6 0.1 copy.70
  79.7 0.1 copy.71
  79.8 1.3 multiply_convert_fusion.1
  81.1 2.7 %copy.72 = bf16[32,32,128]{2,1,0:T(8,128)(2,1)S(1)} copy(bf16[32,32,128]{0,1,2:T(8,128)(2,1)} %multiply_convert_fusion.1) | data formatting | bytes 524288 | tf_op jit(solution)/shard_map/convert_element_type | solution.py:26
  83.8 0.4 fusion.60
  84.1 0.4 multiply_reduce_fusion.3
  84.5 0.3 multiply_convert_fusion.3
  84.9 0.3 fusion.49
  85.2 0.3 fusion.51
  85.5 1.0 fusion.20
  86.5 0.1 copy.73
  86.7 13.1 %all_to_all.48 = bf16[32,32,128]{2,0,1:T(8,128)(2,1)S(1)} all-to-all(bf16[32,32,128]{2,0,1:T(8,128)(2,1)S(1)} %copy.73), channel_id=1, replica_groups=mesh['row'=4,'col'=4,'crop'=2] {'col'}, dimensions={1} | all-to-all | bytes 524288 | tf_op jit(solution)/shard_map/all_to_all | solution.py:67
  99.8 8.2 %all_to_all.49 = bf16[32,32,128]{2,0,1:T(8,128)(2,1)S(1)} all-to-all(bf16[32,32,128]{2,0,1:T(8,128)(2,1)S(1)} %all_to_all.48), channel_id=1, replica_groups=mesh['row'=4,'col'=4,'crop'=2] {'row'}, dimensions={1} | all-to-all | bytes 524288 | tf_op jit(solution)/shard_map/all_to_all | solution.py:66
  108.0 0.1 copy.75
  108.1 0.9 copy.76
  109.1 1.1 fusion.3
  110.2 3.4 %all-gather.9.cloned.1.call-done = bf16[128,32,128]{2,1,0:T(8,128)(2,1)} async-done(((bf16[32,32,128]{2,1,0:T(8,128)(2,1)}), bf16[128,32,128]{2,1,0:T(8,128)(2,1)}) %all-gather.9.cloned.1.call-update) | async-done | bytes 1048592 | tf_op jit(solution)/shard_map/all_gather | solution.py:74
  113.6 3.2 %copy.77 = bf16[128,32,128]{0,1,2:T(8,128)(2,1)} copy(bf16[128,32,128]{2,1,0:T(8,128)(2,1)} %all-gather.9.cloned.1.call-done) | data formatting | bytes 2097152 | tf_op jit(solution)/shard_map/all_gather | solution.py:74
  116.8 27.7 %all-gather.11.cloned.1.call-done = bf16[128,32,128]{0,1,2:T(8,128)(2,1)} async-done(((bf16[128,8,128]{0,1,2:T(8,128)(2,1)}), bf16[128,32,128]{0,1,2:T(8,128)(2,1)}) %all-gather.11.cloned.1.call-update) | async-done | bytes 1048592 | tf_op jit(solution)/shard_map/all_gather | solution.py:77
  144.5 2.2 %bitcast_reduce_fusion = (f32[32,32]{0,1:T(8,128)S(1)}, f32[128,32,32]{2,1,0:T(8,128)S(1)}) fusion(bf16[128,32,128]{0,1,2:T(8,128)(2,1)} %copy.77, bf16[128,32,128]{0,1,2:T(8,128)(2,1)} %all-gather.11.cloned.1.call-done), kind=kOutput, calls=%fused_computation.3 | convolution fusion | flops 33684480 | bytes 2625536 | tf_op jit(solution)/shard_map/kih,kjh->ijh/dot_general | solution.py:75
  146.7 0.1 copy.78
  146.8 0.1 copy.79
  146.9 0.3 multiply_reduce_fusion
  147.2 0.1 copy.80
  147.3 0.1 copy.81
  147.4 1.3 multiply_convert_fusion
  148.6 2.6 %copy.82 = bf16[32,32,128]{2,1,0:T(8,128)(2,1)S(1)} copy(bf16[32,32,128]{0,1,2:T(8,128)(2,1)} %multiply_convert_fusion) | data formatting | bytes 524288 | tf_op jit(solution)/shard_map/convert_element_type | solution.py:26
  151.3 1.4 fusion.61
  152.7 0.4 multiply_reduce_fusion.2
  153.1 0.8 fusion.39
  153.9 0.1 copy-done.7
  154.0 1.4 fusion.13
  (39 shorter events, 0.3 us)
Async XLA Ops:
  6.5 146.6 %copy-start = (bf16[128,1024]{1,0:T(8,128)(2,1)S(1)}, bf16[128,1024]{1,0:T(8,128)(2,1)}, u32[]{:S(2)}) copy-start(bf16[128,1024]{1,0:T(8,128)(2,1)} %param.22) | copy-start | bytes 786436
  6.5 4.0 %copy-start.1 = (bf16[32,32,128]{2,1,0:T(8,128)(2,1)S(1)}, bf16[32,32,128]{2,1,0:T(8,128)(2,1)}, u32[]{:S(2)}) copy-start(bf16[32,32,128]{2,1,0:T(8,128)(2,1)} %param.12) | copy-start | bytes 786436
  6.5 5.3 %copy-start.6 = (s32[32,32]{1,0:T(8,128)S(1)}, s32[32,32]{1,0:T(8,128)}, u32[]{:S(2)}) copy-start(s32[32,32]{1,0:T(8,128)} %param.13) | copy-start | bytes 12292
  6.5 43.3 %all-gather.7.cloned.1.call-start = ((), (), s32[]{:S(2)}) async-start(), calls=%async_computation.5 | async-start | bytes 1310720 | tf_op jit(solution)/shard_map/all_gather | solution.py:56
  11.9 33.8 %copy-start.8 = (bf16[128,128]{1,0:T(8,128)(2,1)S(1)}, bf16[128,128]{1,0:T(8,128)(2,1)}, u32[]{:S(2)}) copy-start(bf16[128,128]{1,0:T(8,128)(2,1)} %param.16) | copy-start | bytes 98308
  12.9 64.0 %all-gather.5.cloned.1.call-start = ((), (), s32[]{:S(2)}) async-start(), calls=%async_computation.4 | async-start | bytes 1310720 | tf_op jit(solution)/shard_map/all_gather | solution.py:60
  45.7 67.9 %all-gather.9.cloned.1.call-start = ((), (), s32[]{:S(2)}) async-start(), calls=%async_computation.6 | async-start | bytes 1310720 | tf_op jit(solution)/shard_map/all_gather | solution.py:74
  79.8 3.9 %copy-start.5 = (bf16[128,128]{1,0:T(8,128)(2,1)S(1)}, bf16[128,128]{1,0:T(8,128)(2,1)}, u32[]{:S(2)}) copy-start(bf16[128,128]{1,0:T(8,128)(2,1)} %param.17) | copy-start | bytes 98308
  81.1 3.8 %copy-start.2 = (bf16[128,256]{1,0:T(8,128)(2,1)S(1)}, bf16[128,256]{1,0:T(8,128)(2,1)}, u32[]{:S(2)}) copy-start(bf16[128,256]{1,0:T(8,128)(2,1)} %param.18) | copy-start | bytes 196612
  83.7 1.4 copy-start.3
  86.5 22.6 %copy-start.9 = (bf16[128,128]{1,0:T(8,128)(2,1)S(1)}, bf16[128,128]{1,0:T(8,128)(2,1)}, u32[]{:S(2)}) copy-start(bf16[128,128]{1,0:T(8,128)(2,1)} %param.20) | copy-start | bytes 98308
  86.5 58.0 %all-gather.11.cloned.1.call-start = ((), (), s32[]{:S(2)}) async-start(), calls=%async_computation.7 | async-start | bytes 1310720 | tf_op jit(solution)/shard_map/all_gather | solution.py:77
  147.4 3.9 %copy-start.4 = (bf16[128,128]{1,0:T(8,128)(2,1)S(1)}, bf16[128,128]{1,0:T(8,128)(2,1)}, u32[]{:S(2)}) copy-start(bf16[128,128]{1,0:T(8,128)(2,1)} %param.21) | copy-start | bytes 98308
  153.1 0.9 copy-start.7
Sparse Core Ops, SparseCore 0:
  13.1 36.7 all-gather.6
  51.7 25.2 all-gather.4
  86.6 26.9 all-gather.8
  115.0 29.4 all-gather.10
where the time goes:
time: 163 us; the launch traced here: 162 us
  waiting for transfers between devices  59 us (36%)
  blocking collectives  53.1 us (33%)
  local copies, waits for them, and re-layouts  14 us (9%)
  matrix products  13.4 us (8%)
  between operations  13.4 us (8%)
  other arithmetic  8.94 us (5%)
    all_gather x1, waiting for transfers between devices, shards(): lax.all_gather(turned_left, 'col', axis=1, tiled=True)  27.7 us
    all_gather x1, waiting for transfers between devices, shards(): lax.all_gather(turned_right, 'row', axis=0, tiled=True)  24.4 us
    all_to_all x1, blocking collectives, shards(): lax.all_to_all(lax.all_to_all(outbound, 'row', split_axis=0, concat_axis=...  21 us
    all_to_all x1, blocking collectives, shards(): lax.all_to_all(outbound_left, 'col', split_axis=1, concat_axis=1, tiled=T...  13.1 us
    all_to_all x1, blocking collectives, shards(): lax.all_to_all(outbound, 'row', split_axis=0, concat_axis=0, tiled=True)  10.7 us
    all_to_all x1, blocking collectives, shards(): lax.all_to_all(lax.all_to_all(outbound_left, 'col', split_axis=1, concat_...  8.25 us
    convert_element_type x2, local copies, waits for them, and re-layouts, finish(): tri_norm = layer_norm(triangle).astype(jnp.bfloat16)  5.27 us
    all_gather x1, waiting for transfers between devices, shards(): column_panel = lax.all_gather(right_tile, 'row', axis=0, tiled=True)  3.41 us
  transfers between devices with their start and end apart: 4, of which 4 were waited for; matrix products, arithmetic and copies ran while one was open for 6% of the time, Pallas kernels for 0%

commit v1 on v0

--- a/solution.py
+++ b/solution.py
@@ -74,7 +74,7 @@
     column_panel = lax.all_gather(right_tile, "row", axis=0, tiled=True)
     triangle_in = jnp.einsum(
         "kih,kjh->ijh",
-        lax.all_gather(turned_left, "col", axis=1, tiled=True),
+        jnp.concatenate(lax.all_gather(turned_left, "col"), axis=1),
         column_panel,
         preferred_element_type=jnp.float32,
     )

time: 163 us -> 164 us (level)
  local copies, waits for them, and re-layouts: 14 us -> 16.6 us
  waiting for transfers between devices: 59 us -> 57.3 us
    reshape x0 -> x1, local copies, waits for them, and re-layouts: none -> 2.93 us  [shards(): jnp.concatenate(lax.all_gather(turned_left, 'col'), axis=1)]
    all_gather x1, waiting for transfers between devices: 27.7 us -> 25.8 us  [shards(): lax.all_gather(turned_left, 'col')]
where the time goes in v1:
time: 164 us; the launch traced here: 163 us
  waiting for transfers between devices  57.3 us (35%)
  blocking collectives  53.1 us (32%)
  local copies, waits for them, and re-layouts  16.6 us (10%)
  matrix products  13.4 us (8%)
  between operations  13.4 us (8%)
  other arithmetic  8.93 us (5%)
    all_gather x1, waiting for transfers between devices, shards(): lax.all_gather(turned_left, 'col')  25.8 us
    all_gather x1, waiting for transfers between devices, shards(): lax.all_gather(turned_right, 'row', axis=0, tiled=True)  24.4 us
    all_to_all x1, blocking collectives, shards(): lax.all_to_all(lax.all_to_all(outbound, 'row', split_axis=0, concat_axis=...  21 us
    all_to_all x1, blocking collectives, shards(): lax.all_to_all(outbound_left, 'col', split_axis=1, concat_axis=1, tiled=T...  13.1 us
    all_to_all x1, blocking collectives, shards(): lax.all_to_all(outbound, 'row', split_axis=0, concat_axis=0, tiled=True)  10.7 us
    all_to_all x1, blocking collectives, shards(): lax.all_to_all(lax.all_to_all(outbound_left, 'col', split_axis=1, concat_...  8.25 us
    convert_element_type x2, local copies, waits for them, and re-layouts, finish(): tri_norm = layer_norm(triangle).astype(jnp.bfloat16)  5.27 us
    all_gather x1, waiting for transfers between devices, shards(): column_panel = lax.all_gather(right_tile, 'row', axis=0, tiled=True)  3.65 us
  transfers between devices with their start and end apart: 4, of which 4 were waited for; matrix products, arithmetic and copies ran while one was open for 6% of the time, Pallas kernels for 0%

profile of v1, /device:TPU:0, one launch (start us, length us, event | category | flops | bytes accessed | tf_op | source)
XLA Modules:
  0.0 162.9 jit_solution(3213414092409150214)
XLA Ops:
  6.5 1.2 convert_reduce_fusion
  7.8 1.3 fusion.19
  9.1 1.4 fusion.46
  10.6 1.3 fusion.48
  11.9 1.0 fusion.32
  13.0 10.7 %all_to_all.43 = bf16[32,32,128]{2,1,0:T(8,128)(2,1)S(1)} all-to-all(bf16[32,32,128]{2,1,0:T(8,128)(2,1)S(1)} %get-tuple-element.8), channel_id=1, replica_groups=mesh['row'=4,'col'=4,'crop'=2] {'row'}, dimensions={0} | all-to-all | bytes 524288 | tf_op jit(solution)/shard_map/all_to_all | solution.py:49
  23.7 21.0 %all_to_all.44 = bf16[32,32,128]{2,1,0:T(8,128)(2,1)S(1)} all-to-all(bf16[32,32,128]{2,1,0:T(8,128)(2,1)S(1)} %all_to_all.43), channel_id=1, replica_groups=mesh['row'=4,'col'=4,'crop'=2] {'col'}, dimensions={0} | all-to-all | bytes 524288 | tf_op jit(solution)/shard_map/all_to_all | solution.py:48
  44.7 0.9 copy.65
  45.7 0.7 fusion.6
  46.5 3.4 %all-gather.7.cloned.1.call-done = bf16[32,128,128]{2,1,0:T(8,128)(2,1)} async-done(((bf16[32,32,128]{2,1,0:T(8,128)(2,1)}), bf16[32,128,128]{2,1,0:T(8,128)(2,1)}) %all-gather.7.cloned.1.call-update) | async-done | bytes 1048592 | tf_op jit(solution)/shard_map/all_gather | solution.py:56
  49.9 2.7 %copy.66 = bf16[32,128,128]{1,0,2:T(8,128)(2,1)} copy(bf16[32,128,128]{2,1,0:T(8,128)(2,1)} %all-gather.7.cloned.1.call-done) | data formatting | bytes 2097152 | tf_op jit(solution)/shard_map/all_gather | solution.py:56
  52.5 24.4 %all-gather.5.cloned.1.call-done = bf16[32,128,128]{1,0,2:T(8,128)(2,1)} async-done(((bf16[8,128,128]{1,0,2:T(8,128)(2,1)}), bf16[32,128,128]{1,0,2:T(8,128)(2,1)}) %all-gather.5.cloned.1.call-update) | async-done | bytes 1048592 | tf_op jit(solution)/shard_map/all_gather | solution.py:60
  76.9 2.2 %bitcast_reduce_fusion.1 = (f32[32,32]{0,1:T(8,128)S(1)}, f32[128,32,32]{2,1,0:T(8,128)S(1)}) fusion(bf16[32,128,128]{1,0,2:T(8,128)(2,1)} %all-gather.5.cloned.1.call-done, bf16[32,128,128]{1,0,2:T(8,128)(2,1)} %copy.66), kind=kOutput, calls=%fused_computation.5 | convolution fusion | flops 33684480 | bytes 2625536 | tf_op jit(solution)/shard_map/ikh,jkh->ijh/dot_general | solution.py:57
  79.2 0.1 copy.67
  79.2 0.1 copy.68
  79.3 0.3 multiply_reduce_fusion.1
  79.6 0.1 copy.69
  79.7 0.1 copy.70
  79.8 1.3 multiply_convert_fusion.1
  81.1 2.7 %copy.71 = bf16[32,32,128]{2,1,0:T(8,128)(2,1)S(1)} copy(bf16[32,32,128]{0,1,2:T(8,128)(2,1)} %multiply_convert_fusion.1) | data formatting | bytes 524288 | tf_op jit(solution)/shard_map/convert_element_type | solution.py:26
  83.8 0.4 fusion.62
  84.1 0.4 multiply_reduce_fusion.3
  84.5 0.3 multiply_convert_fusion.3
  84.9 0.3 fusion.51
  85.2 0.3 fusion.53
  85.5 1.0 fusion.22
  86.6 0.1 copy.72
  86.7 13.1 %all_to_all.45 = bf16[32,32,128]{2,0,1:T(8,128)(2,1)S(1)} all-to-all(bf16[32,32,128]{2,0,1:T(8,128)(2,1)S(1)} %copy.72), channel_id=1, replica_groups=mesh['row'=4,'col'=4,'crop'=2] {'col'}, dimensions={1} | all-to-all | bytes 524288 | tf_op jit(solution)/shard_map/all_to_all | solution.py:67
  99.8 8.2 %all_to_all.46 = bf16[32,32,128]{2,0,1:T(8,128)(2,1)S(1)} all-to-all(bf16[32,32,128]{2,0,1:T(8,128)(2,1)S(1)} %all_to_all.45), channel_id=1, replica_groups=mesh['row'=4,'col'=4,'crop'=2] {'row'}, dimensions={1} | all-to-all | bytes 524288 | tf_op jit(solution)/shard_map/all_to_all | solution.py:66
  108.0 0.8 copy.74
  108.9 1.1 fusion.3
  109.9 3.7 %all-gather.9.cloned.1.call-done = bf16[128,32,128]{2,1,0:T(8,128)(2,1)} async-done(((bf16[32,32,128]{2,1,0:T(8,128)(2,1)}), bf16[128,32,128]{2,1,0:T(8,128)(2,1)}) %all-gather.9.cloned.1.call-update) | async-done | bytes 1048592 | tf_op jit(solution)/shard_map/all_gather | solution.py:74
  113.6 3.2 %copy.76 = bf16[128,32,128]{0,1,2:T(8,128)(2,1)} copy(bf16[128,32,128]{2,1,0:T(8,128)(2,1)} %all-gather.9.cloned.1.call-done) | data formatting | bytes 2097152 | tf_op jit(solution)/shard_map/all_gather | solution.py:74
  116.8 25.8 %all-gather.11.cloned.1.call-done = bf16[4,128,8,128]{3,2,1,0:T(8,128)(2,1)} async-done(((bf16[1,128,8,128]{3,2,1,0:T(8,128)(2,1)}), bf16[4,128,8,128]{3,2,1,0:T(8,128)(2,1)}) %all-gather.11.cloned.1.call-update) | async-done | bytes 1048592 | tf_op jit(solution)/shard_map/all_gather | solution.py:77
  142.6 2.9 %copy.75 = bf16[128,4,8,128]{0,2,1,3:T(8,128)(2,1)} copy(bf16[128,4,8,128]{3,2,0,1:T(8,128)(2,1)} %bitcast.70) | data formatting | bytes 2097152 | tf_op jit(solution)/shard_map/reshape | solution.py:77
  145.5 2.2 %bitcast_reduce_fusion = (f32[32,32]{0,1:T(8,128)S(1)}, f32[128,32,32]{2,1,0:T(8,128)S(1)}) fusion(bf16[128,32,128]{0,1,2:T(8,128)(2,1)} %copy.76, bf16[128,4,8,128]{0,2,1,3:T(8,128)(2,1)} %copy.75), kind=kOutput, calls=%fused_computation.3 | convolution fusion | flops 33684480 | bytes 2625536 | tf_op jit(solution)/shard_map/kih,kjh->ijh/dot_general | solution.py:75
  147.7 0.1 copy.77
  147.8 0.1 copy.78
  147.9 0.3 multiply_reduce_fusion
  148.2 0.1 copy.79
  148.3 0.1 copy.80
  148.4 1.3 multiply_convert_fusion
  149.7 2.6 %copy.81 = bf16[32,32,128]{2,1,0:T(8,128)(2,1)S(1)} copy(bf16[32,32,128]{0,1,2:T(8,128)(2,1)} %multiply_convert_fusion) | data formatting | bytes 524288 | tf_op jit(solution)/shard_map/convert_element_type | solution.py:26
  152.3 1.4 fusion.63
  153.7 0.4 multiply_reduce_fusion.2
  154.1 0.8 fusion.41
  154.9 0.1 copy-done.7
  155.0 1.4 fusion.13
  (39 shorter events, 0.3 us)
Async XLA Ops:
  6.5 147.6 %copy-start = (bf16[128,1024]{1,0:T(8,128)(2,1)S(1)}, bf16[128,1024]{1,0:T(8,128)(2,1)}, u32[]{:S(2)}) copy-start(bf16[128,1024]{1,0:T(8,128)(2,1)} %param.22) | copy-start | bytes 786436
  6.5 4.0 %copy-start.1 = (bf16[32,32,128]{2,1,0:T(8,128)(2,1)S(1)}, bf16[32,32,128]{2,1,0:T(8,128)(2,1)}, u32[]{:S(2)}) copy-start(bf16[32,32,128]{2,1,0:T(8,128)(2,1)} %param.12) | copy-start | bytes 786436
  6.5 5.3 %copy-start.6 = (s32[32,32]{1,0:T(8,128)S(1)}, s32[32,32]{1,0:T(8,128)}, u32[]{:S(2)}) copy-start(s32[32,32]{1,0:T(8,128)} %param.13) | copy-start | bytes 12292
  6.5 43.3 %all-gather.7.cloned.1.call-start = ((), (), s32[]{:S(2)}) async-start(), calls=%async_computation.5 | async-start | bytes 1310720 | tf_op jit(solution)/shard_map/all_gather | solution.py:56
  11.9 33.8 %copy-start.8 = (bf16[128,128]{1,0:T(8,128)(2,1)S(1)}, bf16[128,128]{1,0:T(8,128)(2,1)}, u32[]{:S(2)}) copy-start(bf16[128,128]{1,0:T(8,128)(2,1)} %param.16) | copy-start | bytes 98308
  12.9 64.0 %all-gather.5.cloned.1.call-start = ((), (), s32[]{:S(2)}) async-start(), calls=%async_computation.4 | async-start | bytes 1310720 | tf_op jit(solution)/shard_map/all_gather | solution.py:60
  45.7 67.9 %all-gather.9.cloned.1.call-start = ((), (), s32[]{:S(2)}) async-start(), calls=%async_computation.6 | async-start | bytes 1310720 | tf_op jit(solution)/shard_map/all_gather | solution.py:74
  79.8 3.9 %copy-start.5 = (bf16[128,128]{1,0:T(8,128)(2,1)S(1)}, bf16[128,128]{1,0:T(8,128)(2,1)}, u32[]{:S(2)}) copy-start(bf16[128,128]{1,0:T(8,128)(2,1)} %param.17) | copy-start | bytes 98308
  81.1 3.8 %copy-start.2 = (bf16[128,256]{1,0:T(8,128)(2,1)S(1)}, bf16[128,256]{1,0:T(8,128)(2,1)}, u32[]{:S(2)}) copy-start(bf16[128,256]{1,0:T(8,128)(2,1)} %param.18) | copy-start | bytes 196612
  83.7 1.4 copy-start.3
  85.5 23.4 %copy-start.9 = (bf16[128,128]{1,0:T(8,128)(2,1)S(1)}, bf16[128,128]{1,0:T(8,128)(2,1)}, u32[]{:S(2)}) copy-start(bf16[128,128]{1,0:T(8,128)(2,1)} %param.20) | copy-start | bytes 98308
  86.5 56.1 %all-gather.11.cloned.1.call-start = ((), (), s32[]{:S(2)}) async-start(), calls=%async_computation.7 | async-start | bytes 1310720 | tf_op jit(solution)/shard_map/all_gather | solution.py:77
  148.4 3.9 %copy-start.4 = (bf16[128,128]{1,0:T(8,128)(2,1)S(1)}, bf16[128,128]{1,0:T(8,128)(2,1)}, u32[]{:S(2)}) copy-start(bf16[128,128]{1,0:T(8,128)(2,1)} %param.21) | copy-start | bytes 98308
  154.1 0.9 copy-start.7
Sparse Core Ops, SparseCore 0:
  13.1 36.7 all-gather.6
  51.7 25.2 all-gather.4
  86.6 26.9 all-gather.8
  115.0 27.5 all-gather.10
